TPU v7x, 128 devices: a whole 4x4x4 slice. The times are simulated.
128 devices in a mesh: blk: 8 (over y, x_lo), inner: 16 (over z, x_hi, core).
Axes of the slice: x: 4 (x_hi: 2, x_lo: 2; x = x_hi * 2 + x_lo), y: 4, z: 4, core: 2. Of those that a mesh axis runs over, the one named last changes fastest.
Arguments:
- points: float32 [16384, 128], P(('blk', 'inner')), may hold values from -8 to 8
- lengthscales: float32 [128], replicated, may hold values from 6 to 24
- noise_level: float32 [1], replicated, may hold values from 1 to 10
- iterate: float32 [16384, 64], P(('blk', 'inner')), may hold values from -6 to 6
- residual: float32 [16384, 64], P(('blk', 'inner')), may hold values from -6 to 6
- direction: float32 [16384, 64], P(('blk', 'inner')), may hold values from -6 to 6
Outputs:
- new_iterate: float32 [16384, 64], P(('blk', 'inner'))
- new_residual: float32 [16384, 64], P(('blk', 'inner'))
- new_direction: float32 [16384, 64], P(('blk', 'inner'))
All inputs are finite; a program needn't handle non-finite values.
Results may differ from a plain program's by a relative error of at most 0.00014.
Values sent between devices are 32-bit elements; how exact they have to be, the bound alone decides.
No kernel may reach another device: no remote copies, remote signals or barrier semaphores. Data moves between devices by JAX's collectives and lax.ppermute only.
A program may use at most 64 MiB of HBM per device.

v0:
```python
import jax
import jax.numpy as jnp
from jax import lax
from jax.sharding import PartitionSpec as P


def sent_together(arrays, axis, dim, along):
    both = jnp.concatenate(arrays, axis=along)
    whole, at, outs = (lax.all_gather(both, axis, axis=dim, tiled=True), 0, [])
    for a in arrays:
        outs.append(lax.slice_in_dim(whole, at, at + a.shape[along], axis=along))
        at += a.shape[along]
    return tuple(outs)


def from_behind(value, axis, by):
    size = lax.axis_size(axis)
    return lax.ppermute(value, axis, [(i, (i + by) % size) for i in range(size)])


def split_up(value, dim, size):
    dims = value.shape
    blocks = value.reshape(*dims[:dim], size, dims[dim] // size, *dims[dim + 1 :])
    return jnp.moveaxis(blocks, dim, 0)


def sum_at_owner(value, axis, dim):
    size = lax.axis_size(axis)
    blocks = lax.all_to_all(split_up(value, dim, size), axis, 0, 0, tiled=True)
    return jnp.sum(blocks, axis=0)


def kernel_block(left, left_sq, right, right_sq):
    products = lax.dot_general(
        left,
        right,
        (((1,), (1,)), ((), ())),
        precision=lax.Precision.HIGHEST,
        preferred_element_type=jnp.float32,
    )
    return jnp.exp(-0.5 * (left_sq[:, None] + right_sq[None, :] - 2.0 * products))


def matmul(left, right):
    return jnp.dot(left, right, precision=lax.Precision.HIGHEST, preferred_element_type=jnp.float32)


def transposed(left, right):
    return lax.dot_general(
        left,
        right,
        (((0,), (0,)), ((), ())),
        precision=lax.Precision.HIGHEST,
        preferred_element_type=jnp.float32,
    )


def chol_solve(matrix, rhs_side):
    factor = jnp.linalg.cholesky(matrix)
    return jax.scipy.linalg.cho_solve((factor, True), rhs_side)


def on_device(points, lengthscales, noise_level, iterate, residual, direction):
    scaled = points / lengthscales[None, :]
    sq_norms = jnp.sum(scaled * scaled, axis=1)
    cycle_size = lax.axis_size("blk")
    group_pts, group_dir = sent_together((scaled, direction), "inner", 0, 1)
    group_sq = jnp.sum(group_pts * group_pts, axis=1)
    partial_value = jnp.zeros((group_pts.shape[0], direction.shape[1]), jnp.float32)
    halfway = cycle_size // 2
    visitor = (scaled, sq_norms, direction, jnp.zeros_like(direction))
    returned = jnp.zeros_like(direction)
    for offset in range(halfway + 1):
        if offset > 0:
            visitor = from_behind((visitor[0], visitor[1], visitor[2], visitor[3]), "blk", 1)
        kernel_tile = kernel_block(group_pts, group_sq, visitor[0], visitor[1])
        partial_value = partial_value + matmul(kernel_tile, visitor[2])
        if 1 <= offset <= halfway - 1:
            carried = visitor[3] + transposed(kernel_tile, group_dir)
            visitor = (visitor[0], visitor[1], visitor[2], carried)
            if offset == halfway - 1:
                returned = from_behind(carried, "blk", -(halfway - 1))
    owned = sum_at_owner(partial_value, "inner", 0)
    image = owned + returned + noise_level[0] * direction
    local_gram = transposed(direction, image)
    local_res = transposed(residual, residual)
    local_cross = transposed(image, residual)
    local_image = transposed(image, image)
    gram_raw, res_gram, cross_gram, image_gram = lax.psum(
        (local_gram, local_res, local_cross, local_image), ("blk", "inner")
    )
    gram_matrix = 0.5 * (gram_raw + gram_raw.T)
    step_size = chol_solve(gram_matrix, res_gram)
    new_residual = residual - matmul(image, step_size)
    cross_term = transposed(step_size, cross_gram)
    new_gram = (
        res_gram - cross_term - cross_term.T + transposed(step_size, matmul(image_gram, step_size))
    )
    new_iterate = iterate + matmul(direction, step_size)
    correction = chol_solve(res_gram, new_gram)
    new_direction = new_residual + matmul(direction, correction)
    return (new_iterate, new_residual, new_direction)


def solution(mesh):
    return jax.shard_map(
        on_device,
        mesh=mesh,
        in_specs=(
            P(("blk", "inner"), None),
            P(),
            P(),
            P(("blk", "inner"), None),
            P(("blk", "inner"), None),
            P(("blk", "inner"), None),
        ),
        out_specs=(P(("blk", "inner"), None), P(("blk", "inner"), None), P(("blk", "inner"), None)),
        check_vma=False,
    )
```

profile of v0, /device:TPU:0, one launch (start us, length us, event | category | flops | bytes accessed | tf_op | source)
XLA Modules:
  0.0 288.0 jit_solution(3452829028754681316)
XLA Ops:
  9.7 1.7 collective-permute-start.1
  11.4 4.8 %collective-permute-done.1 = f32[128,128]{1,0:T(8,128)S(1)} collective-permute-done((f32[128,128]{1,0:T(8,128)S(1)}, f32[128,128]{1,0:T(8,128)S(1)}, u32[]{:S(2)}, u32[]{:S(2)}) %collective-permute-start.1) | collective-permute-done | bytes 65568 | tf_op jit(solution)/shard_map/ppermute | solution.py:18
  16.2 1.9 collective-permute-start.2
  18.1 4.8 %collective-permute-done.2 = f32[128,64]{0,1:T(8,128)S(1)} collective-permute-done((f32[128,64]{0,1:T(8,128)}, f32[128,64]{0,1:T(8,128)S(1)}, u32[]{:S(2)}, u32[]{:S(2)}) %collective-permute-start.2) | collective-permute-done | bytes 32800 | tf_op jit(solution)/shard_map/ppermute | solution.py:18
  23.7 5.5 %collective-permute-done.5 = f32[128,64]{0,1:T(8,128)S(1)} collective-permute-done((f32[128,64]{0,1:T(8,128)S(1)}, f32[128,64]{0,1:T(8,128)S(1)}, u32[]{:S(2)}, u32[]{:S(2)}) %collective-permute-start.5) | collective-permute-done | bytes 32800 | tf_op jit(solution)/shard_map/ppermute | solution.py:18
  29.3 6.1 %collective-permute-done = f32[128]{0:T(128)S(1)} collective-permute-done((f32[128]{0:T(128)S(1)}, f32[128]{0:T(128)S(1)}, u32[]{:S(2)}, u32[]{:S(2)}) %collective-permute-start) | collective-permute-done | bytes 544 | tf_op jit(solution)/shard_map/ppermute | solution.py:18
  35.4 5.7 %collective-permute-done.3 = f32[128]{0:T(128)S(1)} collective-permute-done((f32[128]{0:T(128)S(1)}, f32[128]{0:T(128)S(1)}, u32[]{:S(2)}, u32[]{:S(2)}) %collective-permute-start.3) | collective-permute-done | bytes 544 | tf_op jit(solution)/shard_map/ppermute | solution.py:18
  41.1 5.7 %collective-permute-done.6 = f32[128]{0:T(128)S(1)} collective-permute-done((f32[128]{0:T(128)S(1)}, f32[128]{0:T(128)S(1)}, u32[]{:S(2)}, u32[]{:S(2)}) %collective-permute-start.6) | collective-permute-done | bytes 544 | tf_op jit(solution)/shard_map/ppermute | solution.py:18
  46.8 14.3 %all-gather.2.cloned.1.call-done = f32[2048,192]{1,0:T(8,128)} async-done(((f32[128,192]{1,0:T(8,128)}), f32[2048,192]{1,0:T(8,128)}) %all-gather.2.cloned.1.call-update) | async-done | bytes 1572880 | tf_op jit(solution)/shard_map/all_gather | solution.py:9
  61.2 1.7 multiply_reduce_fusion
  62.9 2.2 convolution_multiply_fusion.3
  65.2 1.1 fusion.2
  66.2 1.3 fusion.67
  67.5 2.2 convolution_add_fusion.5
  69.7 2.0 collective-permute-start.13
  74.7 1.5 convolution_add_fusion.3
  76.2 1.5 convolution_add_fusion.2
  77.7 1.5 convolution_add_fusion.1
  79.2 2.2 fusion.15
  81.4 2.5 collective-permute-start.14
  83.8 1.5 fusion.3
  86.2 4.2 %all-to-all-start = ((f32[16,128,64]{1,2,0:T(8,128)}), f32[16,128,64]{1,2,0:T(8,128)}, u32[]{:S(2)}, u32[]{:S(2)}) async-start(f32[16,128,64]{1,2,0:T(8,128)} %bitcast.82), calls=%async_computation | async-start | bytes 1048576 | tf_op jit(solution)/shard_map/all_to_all | solution.py:29
  90.7 2.2 fusion.18
  92.9 2.1 collective-permute-start.15
  96.5 6.6 %all-to-all-done = f32[16,128,64]{1,2,0:T(8,128)} async-done(((f32[16,128,64]{1,2,0:T(8,128)}), f32[16,128,64]{1,2,0:T(8,128)}, u32[]{:S(2)}, u32[]{:S(2)}) %all-to-all-start) | async-done | bytes 524320 | tf_op jit(solution)/shard_map/all_to_all | solution.py:29
  103.1 1.1 reduce_sum.29
  106.7 140.5 %all-reduce.3.cloned.1.call-done = (f32[64,64]{0,1:T(8,128)}, f32[64,64]{1,0:T(8,128)}, f32[64,64]{1,0:T(8,128)}, f32[64,64]{1,0:T(8,128)}) async-done(((f32[64,64]{0,1:T(8,128)}, f32[64,64]{1,0:T(8,128)}, f32[64,64]{1,0:T(8,128)}, f32[64,64]{1,0:T(8,128)}), (f32[64,64]{0,1:T(8,128)}, f32[64,64]{1,0:T(8,128)}, f32[64,64]{1,0:T(8,128)}, f32[64,64]{1,0:T(8,128)})) %all-reduce.3.cloned.1.call-update) | async-done | bytes 65552 | tf_op jit(solution)/shard_map/psum | solution.py:89
  248.8 5.8 %cholesky.44 = f32[64,64]{1,0:T(8,128)S(1)} custom-call(f32[64,64]{1,0:T(8,128)S(1)} %fusion.58), custom_call_target="Cholesky" | custom-call | tf_op jit(solution)/shard_map/jit(cholesky)/cholesky | solution.py:59
  256.0 4.9 %custom-call.8 = f32[1,64,64]{1,2,0:T(8,128)S(1)} custom-call(f32[1,64,64]{2,1,0:T(8,128)S(1)} %fusion.47), custom_call_target="InvertDiagBlocksLowerTriangular" | custom-call | tf_op jit(solution)/shard_map/jit(_cho_solve)/triangular_solve | solution.py:60
  266.8 5.8 %cholesky.55 = f32[64,64]{1,0:T(8,128)S(1)} custom-call(f32[64,64]{1,0:T(8,128)S(1)} %fusion.53), custom_call_target="Cholesky" | custom-call | tf_op jit(solution)/shard_map/jit(cholesky)/cholesky | solution.py:59
  274.0 4.9 %custom-call.9 = f32[1,64,64]{1,2,0:T(8,128)S(1)} custom-call(f32[1,64,64]{2,1,0:T(8,128)S(1)} %fusion.48), custom_call_target="InvertDiagBlocksLowerTriangular" | custom-call | tf_op jit(solution)/shard_map/jit(_cho_solve)/triangular_solve | solution.py:60
  278.9 1.0 convolution_add_fusion.4
  (70 shorter events, 22.2 us)
Async XLA Ops:
  7.2 54.0 %all-gather.2.cloned.1.call-start = ((), (), s32[]{:S(2)}) async-start(), calls=%async_computation.1 | async-start | bytes 2228224 | tf_op jit(solution)/shard_map/all_gather | solution.py:9
  9.7 6.4 %collective-permute-start.1 = (f32[128,128]{1,0:T(8,128)S(1)}, f32[128,128]{1,0:T(8,128)S(1)}, u32[]{:S(2)}, u32[]{:S(2)}) collective-permute-start(f32[128,128]{1,0:T(8,128)S(1)} %get-tuple-element.10), channel_id=1, source_target_pairs={{0,16},{16,32},{32,48},{48,64},{64,80},{80,96},{96,112},{112,0},{1... | collective-permute-start | bytes 196616 | tf_op jit(solution)/shard_map/ppermute | solution.py:18
  16.2 6.7 %collective-permute-start.4 = (f32[128,128]{1,0:T(8,128)S(1)}, f32[128,128]{1,0:T(8,128)S(1)}, u32[]{:S(2)}, u32[]{:S(2)}) collective-permute-start(f32[128,128]{1,0:T(8,128)S(1)} %collective-permute-done.1), channel_id=1, source_target_pairs={{0,16},{16,32},{32,48},{48,64},{64,80},{80,96},{96,112},{112,0},{1... | collective-permute-start | bytes 196616 | tf_op jit(solution)/shard_map/ppermute | solution.py:18
  16.2 6.7 %collective-permute-start.2 = (f32[128,64]{0,1:T(8,128)}, f32[128,64]{0,1:T(8,128)S(1)}, u32[]{:S(2)}, u32[]{:S(2)}) collective-permute-start(f32[128,64]{0,1:T(8,128)} %param.14), channel_id=1, source_target_pairs={{0,16},{16,32},{32,48},{48,64},{64,80},{80,96},{96,112},{112,0},{1... | collective-permute-start | bytes 98312 | tf_op jit(solution)/shard_map/ppermute | solution.py:18
  22.9 6.4 %collective-permute-start.5 = (f32[128,64]{0,1:T(8,128)S(1)}, f32[128,64]{0,1:T(8,128)S(1)}, u32[]{:S(2)}, u32[]{:S(2)}) collective-permute-start(f32[128,64]{0,1:T(8,128)S(1)} %collective-permute-done.2), channel_id=1, source_target_pairs={{0,16},{16,32},{32,48},{48,64},{64,80},{80,96},{96,112},{112,0},{1... | collective-permute-start | bytes 98312 | tf_op jit(solution)/shard_map/ppermute | solution.py:18
  22.9 23.9 %collective-permute-start.7 = (f32[128,128]{1,0:T(8,128)S(1)}, f32[128,128]{1,0:T(8,128)S(1)}, u32[]{:S(2)}, u32[]{:S(2)}) collective-permute-start(f32[128,128]{1,0:T(8,128)S(1)} %collective-permute-done.4), channel_id=1, source_target_pairs={{0,16},{16,32},{32,48},{48,64},{64,80},{80,96},{96,112},{112,0},{1... | collective-permute-start | bytes 196616 | tf_op jit(solution)/shard_map/ppermute | solution.py:18
  29.3 17.5 %collective-permute-start.8 = (f32[128,64]{0,1:T(8,128)S(1)}, f32[128,64]{0,1:T(8,128)S(1)}, u32[]{:S(2)}, u32[]{:S(2)}) collective-permute-start(f32[128,64]{0,1:T(8,128)S(1)} %collective-permute-done.5), channel_id=1, source_target_pairs={{0,16},{16,32},{32,48},{48,64},{64,80},{80,96},{96,112},{112,0},{1... | collective-permute-start | bytes 98312 | tf_op jit(solution)/shard_map/ppermute | solution.py:18
  29.3 6.1 %collective-permute-start = (f32[128]{0:T(128)S(1)}, f32[128]{0:T(128)S(1)}, u32[]{:S(2)}, u32[]{:S(2)}) collective-permute-start(f32[128]{0:T(128)S(1)} %get-tuple-element.9), channel_id=1, source_target_pairs={{0,16},{16,32},{32,48},{48,64},{64,80},{80,96},{96,112},{112,0},{1... | collective-permute-start | bytes 1544 | tf_op jit(solution)/shard_map/ppermute | solution.py:18
  35.4 5.7 %collective-permute-start.3 = (f32[128]{0:T(128)S(1)}, f32[128]{0:T(128)S(1)}, u32[]{:S(2)}, u32[]{:S(2)}) collective-permute-start(f32[128]{0:T(128)S(1)} %collective-permute-done), channel_id=1, source_target_pairs={{0,16},{16,32},{32,48},{48,64},{64,80},{80,96},{96,112},{112,0},{1... | collective-permute-start | bytes 1544 | tf_op jit(solution)/shard_map/ppermute | solution.py:18
  41.1 5.7 %collective-permute-start.6 = (f32[128]{0:T(128)S(1)}, f32[128]{0:T(128)S(1)}, u32[]{:S(2)}, u32[]{:S(2)}) collective-permute-start(f32[128]{0:T(128)S(1)} %collective-permute-done.3), channel_id=1, source_target_pairs={{0,16},{16,32},{32,48},{48,64},{64,80},{80,96},{96,112},{112,0},{1... | collective-permute-start | bytes 1544 | tf_op jit(solution)/shard_map/ppermute | solution.py:18
  41.1 26.4 %collective-permute-start.12 = (f32[128,64]{0,1:T(8,128)S(1)}, f32[128,64]{0,1:T(8,128)S(1)}, u32[]{:S(2)}, u32[]{:S(2)}) collective-permute-start(f32[128,64]{0,1:T(8,128)S(1)} %broadcast_in_dim.2), channel_id=1, source_target_pairs={{0,16},{16,32},{32,48},{48,64},{64,80},{80,96},{96,112},{112,0},{1... | collective-permute-start | bytes 98312 | tf_op jit(solution)/shard_map/ppermute | solution.py:18
  46.7 37.1 %collective-permute-start.9 = (f32[128]{0:T(128)S(1)}, f32[128]{0:T(128)S(1)}, u32[]{:S(2)}, u32[]{:S(2)}) collective-permute-start(f32[128]{0:T(128)S(1)} %collective-permute-done.6), channel_id=1, source_target_pairs={{0,16},{16,32},{32,48},{48,64},{64,80},{80,96},{96,112},{112,0},{1... | collective-permute-start | bytes 1544 | tf_op jit(solution)/shard_map/ppermute | solution.py:18
  46.7 37.1 %collective-permute-start.11 = (f32[128,64]{0,1:T(8,128)S(1)}, f32[128,64]{0,1:T(8,128)S(1)}, u32[]{:S(2)}, u32[]{:S(2)}) collective-permute-start(f32[128,64]{0,1:T(8,128)S(1)} %collective-permute-done.8), channel_id=1, source_target_pairs={{0,16},{16,32},{32,48},{48,64},{64,80},{80,96},{96,112},{112,0},{1... | collective-permute-start | bytes 98312 | tf_op jit(solution)/shard_map/ppermute | solution.py:18
  46.8 26.9 %collective-permute-start.10 = (f32[128,128]{1,0:T(8,128)S(1)}, f32[128,128]{1,0:T(8,128)S(1)}, u32[]{:S(2)}, u32[]{:S(2)}) collective-permute-start(f32[128,128]{1,0:T(8,128)S(1)} %collective-permute-done.7), channel_id=1, source_target_pairs={{0,16},{16,32},{32,48},{48,64},{64,80},{80,96},{96,112},{112,0},{1... | collective-permute-start | bytes 196616 | tf_op jit(solution)/shard_map/ppermute | solution.py:18
  61.2 4.0 %copy-start = (f32[2048,192]{1,0:T(8,128)S(1)}, f32[2048,192]{1,0:T(8,128)}, u32[]{:S(2)}) copy-start(f32[2048,192]{1,0:T(8,128)} %all-gather.2.cloned.1.call-done) | copy-start | bytes 4718596
  62.9 3.3 %copy-start.1 = (f32[128,64]{0,1:T(8,128)S(1)}, f32[128,64]{0,1:T(8,128)}, u32[]{:S(2)}) copy-start(f32[128,64]{0,1:T(8,128)} %param.14) | copy-start | bytes 98308
  69.7 9.5 %collective-permute-start.13 = (f32[128,64]{0,1:T(8,128)S(1)}, f32[128,64]{0,1:T(8,128)S(1)}, u32[]{:S(2)}, u32[]{:S(2)}) collective-permute-start(f32[128,64]{0,1:T(8,128)S(1)} %convolution_add_fusion.5), channel_id=1, source_target_pairs={{0,16},{16,32},{32,48},{48,64},{64,80},{80,96},{96,112},{112,0},{1... | collective-permute-start | bytes 98312 | tf_op jit(solution)/shard_map/ppermute | solution.py:18
  81.4 9.4 %collective-permute-start.14 = (f32[128,64]{0,1:T(8,128)S(1)}, f32[128,64]{0,1:T(8,128)S(1)}, u32[]{:S(2)}, u32[]{:S(2)}) collective-permute-start(f32[128,64]{0,1:T(8,128)S(1)} %fusion.15), channel_id=1, source_target_pairs={{0,16},{16,32},{32,48},{48,64},{64,80},{80,96},{96,112},{112,0},{1... | collective-permute-start | bytes 98312 | tf_op jit(solution)/shard_map/ppermute | solution.py:18
  85.3 9.7 %copy-start.2 = (f32[128,64]{0,1:T(8,128)S(1)}, f32[128,64]{0,1:T(8,128)}, u32[]{:S(2)}) copy-start(f32[128,64]{0,1:T(8,128)} %param.13) | copy-start | bytes 98308
  86.2 16.9 %all-to-all-start = ((f32[16,128,64]{1,2,0:T(8,128)}), f32[16,128,64]{1,2,0:T(8,128)}, u32[]{:S(2)}, u32[]{:S(2)}) async-start(f32[16,128,64]{1,2,0:T(8,128)} %bitcast.82), calls=%async_computation | async-start | bytes 1048576 | tf_op jit(solution)/shard_map/all_to_all | solution.py:29
  90.4 174.7 %copy-start.4 = (f32[128,64]{0,1:T(8,128)S(1)}, f32[128,64]{0,1:T(8,128)}, u32[]{:S(2)}) copy-start(f32[128,64]{0,1:T(8,128)} %param.12) | copy-start | bytes 98308
  90.5 156.7 %all-reduce.3.cloned.1.call-start = ((), (), s32[]{:S(2)}) async-start(), calls=%async_computation.2 | async-start | bytes 262144 | tf_op jit(solution)/shard_map/psum | solution.py:89
  92.9 11.3 %collective-permute-start.15 = (f32[128,64]{0,1:T(8,128)S(1)}, f32[128,64]{0,1:T(8,128)S(1)}, u32[]{:S(2)}, u32[]{:S(2)}) collective-permute-start(f32[128,64]{0,1:T(8,128)S(1)} %fusion.18), channel_id=1, source_target_pairs={{0,80},{16,96},{32,112},{48,0},{64,16},{80,32},{96,48},{112,64},{1... | collective-permute-start | bytes 98312 | tf_op jit(solution)/shard_map/ppermute | solution.py:18
  263.2 18.0 %copy-start.3 = (f32[128,64]{0,1:T(8,128)}, f32[128,64]{0,1:T(8,128)S(1)}, u32[]{:S(2)}) copy-start(f32[128,64]{0,1:T(8,128)S(1)} %convolution_subtract_fusion) | copy-start | bytes 98308
Sparse Core Ops, SparseCore 0:
  10.4 50.6 all-gather.1
  106.8 140.2 all-reduce.2
where the time goes:
time: 289 us; the launch traced here: 288 us
  waiting for transfers between devices  194 us (67%)
  other arithmetic  30.1 us (10%)
  matrix products  29.6 us (10%)
  starting transfers between devices  15.7 us (5%)
  between operations  15 us (5%)
  local copies, waits for them, and re-layouts  3.56 us (1%)
    psum x1, waiting for transfers between devices, on_device(): lax.psum((local_gram, local_res, local_cross, local_image), ('blk', 'inne...  140 us
    ppermute x16, waiting for transfers between devices, from_behind(): lax.ppermute(value, axis, [(i, (i + by) % size) for i in range(size)])  32.6 us
    all_gather x1, waiting for transfers between devices, sent_together(): whole, at, outs = (lax.all_gather(both, axis, axis=dim, tiled=True), 0, [])  14.3 us
    another operation x6, other arithmetic, chol_solve(): factor = jnp.linalg.cholesky(matrix)  13 us
    dot_general x9, matrix products, transposed(): lax.dot_general(left, right, (((0,), (0,)), ((), ())), precision=lax.Prec...  11.7 us
    ppermute x16, starting transfers between devices, from_behind(): lax.ppermute(value, axis, [(i, (i + by) % size) for i in range(size)])  11.1 us
    another operation x4, other arithmetic, chol_solve(): return jax.scipy.linalg.cho_solve((factor, True), rhs_side)  11.1 us
    dot_general x9, matrix products, matmul(): jnp.dot(left, right, precision=lax.Precision.HIGHEST, preferred_element_t...  10.2 us
  transfers between devices with their start and end apart: 19, of which 9 were waited for; matrix products, arithmetic and copies ran while one was open for 8% of the time, Pallas kernels for 0%

commit v1 on v0

--- a/solution.py
+++ b/solution.py
@@ -87,7 +87,7 @@
     local_cross = transposed(image, residual)
     local_image = transposed(image, image)
     gram_raw, res_gram, cross_gram, image_gram = lax.psum(
-        (local_gram, local_res, local_cross, local_image), ("blk", "inner")
+        lax.psum((local_gram, local_res, local_cross, local_image), "inner"), "blk"
     )
     gram_matrix = 0.5 * (gram_raw + gram_raw.T)
     step_size = chol_solve(gram_matrix, res_gram)

time: 289 us -> 361 us (1.25)
  waiting for transfers between devices: 194 us -> 267 us
    psum x1 -> x2, waiting for transfers between devices: 140 us -> 213 us  [the longest x1 135 us: on_device(): lax.psum((local_gram, local_res, local_cross, local_image), 'inner')]
  transfers between devices with their start and end apart: 19 -> 20, of which waited for: 9 -> 10; matrix products, arithmetic and copies ran while one was open for 8% -> 7% of each run, Pallas kernels for 0% -> 0%
where the time goes in v1:
time: 361 us; the launch traced here: 360 us
  waiting for transfers between devices  267 us (74%)
  other arithmetic  30.1 us (8%)
  matrix products  29.6 us (8%)
  starting transfers between devices  15.7 us (4%)
  between operations  14.7 us (4%)
    psum x1, waiting for transfers between devices, on_device(): lax.psum((local_gram, local_res, local_cross, local_image), 'inner')  135 us
    psum x1, waiting for transfers between devices, on_device(): lax.psum(lax.psum((local_gram, local_res, local_cross, local_image), 'inn...  77.6 us
    ppermute x16, waiting for transfers between devices, from_behind(): lax.ppermute(value, axis, [(i, (i + by) % size) for i in range(size)])  32.6 us
    all_gather x1, waiting for transfers between devices, sent_together(): whole, at, outs = (lax.all_gather(both, axis, axis=dim, tiled=True), 0, [])  14.3 us
    another operation x6, other arithmetic, chol_solve(): factor = jnp.linalg.cholesky(matrix)  13 us
    dot_general x9, matrix products, transposed(): lax.dot_general(left, right, (((0,), (0,)), ((), ())), precision=lax.Prec...  11.7 us
    ppermute x16, starting transfers between devices, from_behind(): lax.ppermute(value, axis, [(i, (i + by) % size) for i in range(size)])  11.1 us
    another operation x4, other arithmetic, chol_solve(): return jax.scipy.linalg.cho_solve((factor, True), rhs_side)  11.1 us
  transfers between devices with their start and end apart: 20, of which 10 were waited for; matrix products, arithmetic and copies ran while one was open for 7% of the time, Pallas kernels for 0%

profile of v1, /device:TPU:0, one launch (start us, length us, event | category | flops | bytes accessed | tf_op | source)
XLA Modules:
  0.0 360.4 jit_solution(1572929728527310335)
XLA Ops:
  9.7 1.7 collective-permute-start.1
  11.4 4.8 %collective-permute-done.1 = f32[128,128]{1,0:T(8,128)S(1)} collective-permute-done((f32[128,128]{1,0:T(8,128)S(1)}, f32[128,128]{1,0:T(8,128)S(1)}, u32[]{:S(2)}, u32[]{:S(2)}) %collective-permute-start.1) | collective-permute-done | bytes 65568 | tf_op jit(solution)/shard_map/ppermute | solution.py:18
  16.2 1.9 collective-permute-start.2
  18.1 4.8 %collective-permute-done.2 = f32[128,64]{0,1:T(8,128)S(1)} collective-permute-done((f32[128,64]{0,1:T(8,128)}, f32[128,64]{0,1:T(8,128)S(1)}, u32[]{:S(2)}, u32[]{:S(2)}) %collective-permute-start.2) | collective-permute-done | bytes 32800 | tf_op jit(solution)/shard_map/ppermute | solution.py:18
  23.7 5.5 %collective-permute-done.5 = f32[128,64]{0,1:T(8,128)S(1)} collective-permute-done((f32[128,64]{0,1:T(8,128)S(1)}, f32[128,64]{0,1:T(8,128)S(1)}, u32[]{:S(2)}, u32[]{:S(2)}) %collective-permute-start.5) | collective-permute-done | bytes 32800 | tf_op jit(solution)/shard_map/ppermute | solution.py:18
  29.3 6.1 %collective-permute-done = f32[128]{0:T(128)S(1)} collective-permute-done((f32[128]{0:T(128)S(1)}, f32[128]{0:T(128)S(1)}, u32[]{:S(2)}, u32[]{:S(2)}) %collective-permute-start) | collective-permute-done | bytes 544 | tf_op jit(solution)/shard_map/ppermute | solution.py:18
  35.4 5.7 %collective-permute-done.3 = f32[128]{0:T(128)S(1)} collective-permute-done((f32[128]{0:T(128)S(1)}, f32[128]{0:T(128)S(1)}, u32[]{:S(2)}, u32[]{:S(2)}) %collective-permute-start.3) | collective-permute-done | bytes 544 | tf_op jit(solution)/shard_map/ppermute | solution.py:18
  41.1 5.7 %collective-permute-done.6 = f32[128]{0:T(128)S(1)} collective-permute-done((f32[128]{0:T(128)S(1)}, f32[128]{0:T(128)S(1)}, u32[]{:S(2)}, u32[]{:S(2)}) %collective-permute-start.6) | collective-permute-done | bytes 544 | tf_op jit(solution)/shard_map/ppermute | solution.py:18
  46.8 14.3 %all-gather.2.cloned.1.call-done = f32[2048,192]{1,0:T(8,128)} async-done(((f32[128,192]{1,0:T(8,128)}), f32[2048,192]{1,0:T(8,128)}) %all-gather.2.cloned.1.call-update) | async-done | bytes 1572880 | tf_op jit(solution)/shard_map/all_gather | solution.py:9
  61.2 1.7 multiply_reduce_fusion
  62.9 2.2 convolution_multiply_fusion.3
  65.2 1.1 fusion.2
  66.2 1.3 fusion.67
  67.5 2.2 convolution_add_fusion.5
  69.7 2.0 collective-permute-start.13
  74.7 1.5 convolution_add_fusion.3
  76.2 1.5 convolution_add_fusion.2
  77.7 1.5 convolution_add_fusion.1
  79.2 2.2 fusion.15
  81.4 2.5 collective-permute-start.14
  83.8 1.5 fusion.3
  86.2 4.3 %all-to-all-start = ((f32[16,128,64]{1,2,0:T(8,128)}), f32[16,128,64]{1,2,0:T(8,128)}, u32[]{:S(2)}, u32[]{:S(2)}) async-start(f32[16,128,64]{1,2,0:T(8,128)} %bitcast.82), calls=%async_computation | async-start | bytes 1048576 | tf_op jit(solution)/shard_map/all_to_all | solution.py:29
  90.7 2.2 fusion.18
  92.9 2.1 collective-permute-start.15
  96.5 6.6 %all-to-all-done = f32[16,128,64]{1,2,0:T(8,128)} async-done(((f32[16,128,64]{1,2,0:T(8,128)}), f32[16,128,64]{1,2,0:T(8,128)}, u32[]{:S(2)}, u32[]{:S(2)}) %all-to-all-start) | async-done | bytes 524320 | tf_op jit(solution)/shard_map/all_to_all | solution.py:29
  103.1 1.1 reduce_sum.29
  106.7 135.4 %all-reduce.5.cloned.1.call-done = (f32[64,64]{0,1:T(8,128)}, f32[64,64]{1,0:T(8,128)}, f32[64,64]{1,0:T(8,128)}, f32[64,64]{1,0:T(8,128)}) async-done(((f32[64,64]{0,1:T(8,128)}, f32[64,64]{1,0:T(8,128)}, f32[64,64]{1,0:T(8,128)}, f32[64,64]{1,0:T(8,128)}), (f32[64,64]{0,1:T(8,128)}, f32[64,64]{1,0:T(8,128)}, f32[64,64]{1,0:T(8,128)}, f32[64,64]{1,0:T(8,128)})) %all-reduce.5.cloned.1.call-update) | async-done | bytes 65552 | tf_op jit(solution)/shard_map/psum | solution.py:90
  242.2 77.6 %all-reduce.7.cloned.1.call-done = (f32[64,64]{0,1:T(8,128)}, f32[64,64]{1,0:T(8,128)}, f32[64,64]{1,0:T(8,128)}, f32[64,64]{1,0:T(8,128)}) async-done(((f32[64,64]{0,1:T(8,128)}, f32[64,64]{1,0:T(8,128)}, f32[64,64]{1,0:T(8,128)}, f32[64,64]{1,0:T(8,128)}), (f32[64,64]{0,1:T(8,128)}, f32[64,64]{1,0:T(8,128)}, f32[64,64]{1,0:T(8,128)}, f32[64,64]{1,0:T(8,128)})) %all-reduce.7.cloned.1.call-update) | async-done | bytes 65552 | tf_op jit(solution)/shard_map/psum | solution.py:89
  321.5 5.8 %cholesky.44 = f32[64,64]{1,0:T(8,128)S(1)} custom-call(f32[64,64]{1,0:T(8,128)S(1)} %fusion.58), custom_call_target="Cholesky" | custom-call | tf_op jit(solution)/shard_map/jit(cholesky)/cholesky | solution.py:59
  328.7 4.9 %custom-call.8 = f32[1,64,64]{1,2,0:T(8,128)S(1)} custom-call(f32[1,64,64]{2,1,0:T(8,128)S(1)} %fusion.47), custom_call_target="InvertDiagBlocksLowerTriangular" | custom-call | tf_op jit(solution)/shard_map/jit(_cho_solve)/triangular_solve | solution.py:60
  339.5 5.8 %cholesky.55 = f32[64,64]{1,0:T(8,128)S(1)} custom-call(f32[64,64]{1,0:T(8,128)S(1)} %fusion.53), custom_call_target="Cholesky" | custom-call | tf_op jit(solution)/shard_map/jit(cholesky)/cholesky | solution.py:59
  346.7 4.9 %custom-call.9 = f32[1,64,64]{1,2,0:T(8,128)S(1)} custom-call(f32[1,64,64]{2,1,0:T(8,128)S(1)} %fusion.48), custom_call_target="InvertDiagBlocksLowerTriangular" | custom-call | tf_op jit(solution)/shard_map/jit(_cho_solve)/triangular_solve | solution.py:60
  (73 shorter events, 23.3 us)
Async XLA Ops:
  7.2 54.0 %all-gather.2.cloned.1.call-start = ((), (), s32[]{:S(2)}) async-start(), calls=%async_computation.1 | async-start | bytes 2228224 | tf_op jit(solution)/shard_map/all_gather | solution.py:9
  9.7 6.4 %collective-permute-start.1 = (f32[128,128]{1,0:T(8,128)S(1)}, f32[128,128]{1,0:T(8,128)S(1)}, u32[]{:S(2)}, u32[]{:S(2)}) collective-permute-start(f32[128,128]{1,0:T(8,128)S(1)} %get-tuple-element.14), channel_id=1, source_target_pairs={{0,16},{16,32},{32,48},{48,64},{64,80},{80,96},{96,112},{112,0},{1... | collective-permute-start | bytes 196616 | tf_op jit(solution)/shard_map/ppermute | solution.py:18
  16.2 6.7 %collective-permute-start.4 = (f32[128,128]{1,0:T(8,128)S(1)}, f32[128,128]{1,0:T(8,128)S(1)}, u32[]{:S(2)}, u32[]{:S(2)}) collective-permute-start(f32[128,128]{1,0:T(8,128)S(1)} %collective-permute-done.1), channel_id=1, source_target_pairs={{0,16},{16,32},{32,48},{48,64},{64,80},{80,96},{96,112},{112,0},{1... | collective-permute-start | bytes 196616 | tf_op jit(solution)/shard_map/ppermute | solution.py:18
  16.2 6.7 %collective-permute-start.2 = (f32[128,64]{0,1:T(8,128)}, f32[128,64]{0,1:T(8,128)S(1)}, u32[]{:S(2)}, u32[]{:S(2)}) collective-permute-start(f32[128,64]{0,1:T(8,128)} %param.14), channel_id=1, source_target_pairs={{0,16},{16,32},{32,48},{48,64},{64,80},{80,96},{96,112},{112,0},{1... | collective-permute-start | bytes 98312 | tf_op jit(solution)/shard_map/ppermute | solution.py:18
  22.9 6.4 %collective-permute-start.5 = (f32[128,64]{0,1:T(8,128)S(1)}, f32[128,64]{0,1:T(8,128)S(1)}, u32[]{:S(2)}, u32[]{:S(2)}) collective-permute-start(f32[128,64]{0,1:T(8,128)S(1)} %collective-permute-done.2), channel_id=1, source_target_pairs={{0,16},{16,32},{32,48},{48,64},{64,80},{80,96},{96,112},{112,0},{1... | collective-permute-start | bytes 98312 | tf_op jit(solution)/shard_map/ppermute | solution.py:18
  22.9 23.9 %collective-permute-start.7 = (f32[128,128]{1,0:T(8,128)S(1)}, f32[128,128]{1,0:T(8,128)S(1)}, u32[]{:S(2)}, u32[]{:S(2)}) collective-permute-start(f32[128,128]{1,0:T(8,128)S(1)} %collective-permute-done.4), channel_id=1, source_target_pairs={{0,16},{16,32},{32,48},{48,64},{64,80},{80,96},{96,112},{112,0},{1... | collective-permute-start | bytes 196616 | tf_op jit(solution)/shard_map/ppermute | solution.py:18
  29.3 17.5 %collective-permute-start.8 = (f32[128,64]{0,1:T(8,128)S(1)}, f32[128,64]{0,1:T(8,128)S(1)}, u32[]{:S(2)}, u32[]{:S(2)}) collective-permute-start(f32[128,64]{0,1:T(8,128)S(1)} %collective-permute-done.5), channel_id=1, source_target_pairs={{0,16},{16,32},{32,48},{48,64},{64,80},{80,96},{96,112},{112,0},{1... | collective-permute-start | bytes 98312 | tf_op jit(solution)/shard_map/ppermute | solution.py:18
  29.3 6.1 %collective-permute-start = (f32[128]{0:T(128)S(1)}, f32[128]{0:T(128)S(1)}, u32[]{:S(2)}, u32[]{:S(2)}) collective-permute-start(f32[128]{0:T(128)S(1)} %get-tuple-element.13), channel_id=1, source_target_pairs={{0,16},{16,32},{32,48},{48,64},{64,80},{80,96},{96,112},{112,0},{1... | collective-permute-start | bytes 1544 | tf_op jit(solution)/shard_map/ppermute | solution.py:18
  35.4 5.7 %collective-permute-start.3 = (f32[128]{0:T(128)S(1)}, f32[128]{0:T(128)S(1)}, u32[]{:S(2)}, u32[]{:S(2)}) collective-permute-start(f32[128]{0:T(128)S(1)} %collective-permute-done), channel_id=1, source_target_pairs={{0,16},{16,32},{32,48},{48,64},{64,80},{80,96},{96,112},{112,0},{1... | collective-permute-start | bytes 1544 | tf_op jit(solution)/shard_map/ppermute | solution.py:18
  41.1 5.7 %collective-permute-start.6 = (f32[128]{0:T(128)S(1)}, f32[128]{0:T(128)S(1)}, u32[]{:S(2)}, u32[]{:S(2)}) collective-permute-start(f32[128]{0:T(128)S(1)} %collective-permute-done.3), channel_id=1, source_target_pairs={{0,16},{16,32},{32,48},{48,64},{64,80},{80,96},{96,112},{112,0},{1... | collective-permute-start | bytes 1544 | tf_op jit(solution)/shard_map/ppermute | solution.py:18
  41.1 26.4 %collective-permute-start.12 = (f32[128,64]{0,1:T(8,128)S(1)}, f32[128,64]{0,1:T(8,128)S(1)}, u32[]{:S(2)}, u32[]{:S(2)}) collective-permute-start(f32[128,64]{0,1:T(8,128)S(1)} %broadcast_in_dim.2), channel_id=1, source_target_pairs={{0,16},{16,32},{32,48},{48,64},{64,80},{80,96},{96,112},{112,0},{1... | collective-permute-start | bytes 98312 | tf_op jit(solution)/shard_map/ppermute | solution.py:18
  46.7 37.1 %collective-permute-start.9 = (f32[128]{0:T(128)S(1)}, f32[128]{0:T(128)S(1)}, u32[]{:S(2)}, u32[]{:S(2)}) collective-permute-start(f32[128]{0:T(128)S(1)} %collective-permute-done.6), channel_id=1, source_target_pairs={{0,16},{16,32},{32,48},{48,64},{64,80},{80,96},{96,112},{112,0},{1... | collective-permute-start | bytes 1544 | tf_op jit(solution)/shard_map/ppermute | solution.py:18
  46.7 37.1 %collective-permute-start.11 = (f32[128,64]{0,1:T(8,128)S(1)}, f32[128,64]{0,1:T(8,128)S(1)}, u32[]{:S(2)}, u32[]{:S(2)}) collective-permute-start(f32[128,64]{0,1:T(8,128)S(1)} %collective-permute-done.8), channel_id=1, source_target_pairs={{0,16},{16,32},{32,48},{48,64},{64,80},{80,96},{96,112},{112,0},{1... | collective-permute-start | bytes 98312 | tf_op jit(solution)/shard_map/ppermute | solution.py:18
  46.8 26.9 %collective-permute-start.10 = (f32[128,128]{1,0:T(8,128)S(1)}, f32[128,128]{1,0:T(8,128)S(1)}, u32[]{:S(2)}, u32[]{:S(2)}) collective-permute-start(f32[128,128]{1,0:T(8,128)S(1)} %collective-permute-done.7), channel_id=1, source_target_pairs={{0,16},{16,32},{32,48},{48,64},{64,80},{80,96},{96,112},{112,0},{1... | collective-permute-start | bytes 196616 | tf_op jit(solution)/shard_map/ppermute | solution.py:18
  61.2 4.0 %copy-start = (f32[2048,192]{1,0:T(8,128)S(1)}, f32[2048,192]{1,0:T(8,128)}, u32[]{:S(2)}) copy-start(f32[2048,192]{1,0:T(8,128)} %all-gather.2.cloned.1.call-done) | copy-start | bytes 4718596
  62.9 3.3 copy-start.1
  69.7 9.5 %collective-permute-start.13 = (f32[128,64]{0,1:T(8,128)S(1)}, f32[128,64]{0,1:T(8,128)S(1)}, u32[]{:S(2)}, u32[]{:S(2)}) collective-permute-start(f32[128,64]{0,1:T(8,128)S(1)} %convolution_add_fusion.5), channel_id=1, source_target_pairs={{0,16},{16,32},{32,48},{48,64},{64,80},{80,96},{96,112},{112,0},{1... | collective-permute-start | bytes 98312 | tf_op jit(solution)/shard_map/ppermute | solution.py:18
  81.4 9.4 %collective-permute-start.14 = (f32[128,64]{0,1:T(8,128)S(1)}, f32[128,64]{0,1:T(8,128)S(1)}, u32[]{:S(2)}, u32[]{:S(2)}) collective-permute-start(f32[128,64]{0,1:T(8,128)S(1)} %fusion.15), channel_id=1, source_target_pairs={{0,16},{16,32},{32,48},{48,64},{64,80},{80,96},{96,112},{112,0},{1... | collective-permute-start | bytes 98312 | tf_op jit(solution)/shard_map/ppermute | solution.py:18
  85.3 9.7 %copy-start.2 = (f32[128,64]{0,1:T(8,128)S(1)}, f32[128,64]{0,1:T(8,128)}, u32[]{:S(2)}) copy-start(f32[128,64]{0,1:T(8,128)} %param.13) | copy-start | bytes 98308
  86.2 17.0 %all-to-all-start = ((f32[16,128,64]{1,2,0:T(8,128)}), f32[16,128,64]{1,2,0:T(8,128)}, u32[]{:S(2)}, u32[]{:S(2)}) async-start(f32[16,128,64]{1,2,0:T(8,128)} %bitcast.82), calls=%async_computation | async-start | bytes 1048576 | tf_op jit(solution)/shard_map/all_to_all | solution.py:29
  90.4 247.4 %copy-start.4 = (f32[128,64]{0,1:T(8,128)S(1)}, f32[128,64]{0,1:T(8,128)}, u32[]{:S(2)}) copy-start(f32[128,64]{0,1:T(8,128)} %param.12) | copy-start | bytes 98308
  90.5 151.7 %all-reduce.5.cloned.1.call-start = ((), (), s32[]{:S(2)}) async-start(), calls=%async_computation.2 | async-start | bytes 262144 | tf_op jit(solution)/shard_map/psum | solution.py:90
  92.9 11.3 %collective-permute-start.15 = (f32[128,64]{0,1:T(8,128)S(1)}, f32[128,64]{0,1:T(8,128)S(1)}, u32[]{:S(2)}, u32[]{:S(2)}) collective-permute-start(f32[128,64]{0,1:T(8,128)S(1)} %fusion.18), channel_id=1, source_target_pairs={{0,80},{16,96},{32,112},{48,0},{64,16},{80,32},{96,48},{112,64},{1... | collective-permute-start | bytes 98312 | tf_op jit(solution)/shard_map/ppermute | solution.py:18
  106.7 213.1 %all-reduce.7.cloned.1.call-start = ((), (), s32[]{:S(2)}) async-start(), calls=%async_computation.3 | async-start | bytes 262144 | tf_op jit(solution)/shard_map/psum | solution.py:89
  335.8 18.0 %copy-start.3 = (f32[128,64]{0,1:T(8,128)}, f32[128,64]{0,1:T(8,128)S(1)}, u32[]{:S(2)}) copy-start(f32[128,64]{0,1:T(8,128)S(1)} %convolution_subtract_fusion) | copy-start | bytes 98308
Sparse Core Ops, SparseCore 0:
  10.4 50.6 all-gather.1
  106.8 135.3 all-reduce.4
  244.9 74.8 all-reduce.6
